TPU v7x, 128 devices: a whole 4x4x4 slice. The times are simulated.
128 devices in a mesh: fsdp: 8 (over z_hi, y), tp: 16 (over z_lo, x, core).
Axes of the slice: x: 4, y: 4, z: 4 (z_hi: 2, z_lo: 2; z = z_hi * 2 + z_lo), core: 2. Of those that a mesh axis runs over, the one named last changes fastest.
Arguments:
- tokens: bfloat16 [2048, 8192], P('fsdp', 'tp'), may hold values from -6 to 6
- out_grad: bfloat16 [2048, 8192], P('fsdp', 'tp'), may hold values from -6 to 6
- gate_weight: bfloat16 [8192, 2048], P('fsdp', 'tp'), may hold values from -0.0625 to 0.0625
- up_weight: bfloat16 [8192, 2048], P('fsdp', 'tp'), may hold values from -0.0625 to 0.0625
- down_weight: bfloat16 [2048, 8192], P('tp', 'fsdp'), may hold values from -0.125 to 0.125
Outputs:
- input_grad: bfloat16 [2048, 8192], P('fsdp', 'tp')
- gate_grad: float32 [8192, 2048], P('fsdp', 'tp')
- up_grad: float32 [8192, 2048], P('fsdp', 'tp')
- down_grad: float32 [2048, 8192], P('tp', 'fsdp')
All inputs are finite; a program needn't handle non-finite values.
Results may differ from a plain program's by a relative error of at most 0.0023.
Values may be sent and summed in bfloat16 or wider, within the bound.
No kernel may reach another device: no remote copies, remote signals or barrier semaphores. Data moves between devices by JAX's collectives and lax.ppermute only.
A program may use at most 128 MiB of HBM per device.

v0:
```python
import math
import jax
import jax.numpy as jnp
from jax import lax
from jax.sharding import Mesh
from jax.sharding import PartitionSpec as P

FSDP = ("fsdp_0", "fsdp_1")


def laid_out(parts, dim):
    parts = jnp.moveaxis(parts, 0, dim)
    dims = parts.shape
    return parts.reshape(*dims[:dim], dims[dim] * dims[dim + 1], *dims[dim + 2 :])


def one_gather(arrays, axis, dims):
    line = jnp.concatenate([a.reshape(-1) for a in arrays])
    lines, at, outs = (lax.all_gather(line, axis), 0, [])
    for a, dim in zip(arrays, dims):
        parts = lines[:, at : at + a.size].reshape(-1, *a.shape)
        outs.append(laid_out(parts, dim))
        at += a.size
    return tuple(outs)


def stacked_from(value, axes, turns):
    parts = value[None]
    for k in turns:
        parts = lax.all_gather(parts, axes[k], axis=0, tiled=True)
    current = [lax.axis_size(axes[k]) for k in reversed(turns)]
    parts = parts.reshape(*current, *value.shape)
    turned = sorted(range(len(turns)), key=lambda place: turns[len(turns) - 1 - place])
    return parts.transpose(*turned, *range(len(turns), parts.ndim)).reshape(-1, *value.shape)


def gathered_by_axis(value, axes, turns, dim):
    return laid_out(stacked_from(value, axes, turns), dim)


def taken_in(value, axes, turns, dim, absorb, carry):
    everything = jax.tree.map(lambda part: gathered_by_axis(part, axes, turns, dim), value)
    return absorb(carry, everything, jnp.int32(0))


def own_rows(portion, rows, axis):
    count = rows * lax.axis_size(axis)
    return lax.psum_scatter(portion(jnp.int32(0), count), axis, scatter_dimension=0, tiled=True)


def column_term(left, right, start, count, factor):
    block = lax.dynamic_slice_in_dim(left, start, count, 1)
    product = lax.dot_general(
        block, right, (((0,), (0,)), ((), ())), preferred_element_type=jnp.float32
    )
    return product * factor


def shards(tokens, out_grad, gate_weight, up_weight, down_weight):
    factor = 1.0 / math.sqrt(tokens.shape[0] * lax.axis_size(FSDP))
    whole = lax.all_gather(tokens, "tp", axis=1, tiled=True)
    grads = lax.all_gather(out_grad, "tp", axis=1, tiled=True)
    gate_full, up_full = one_gather((gate_weight, up_weight), FSDP, (0, 0))
    gate = jnp.dot(whole, gate_full, preferred_element_type=jnp.float32)
    up = jnp.dot(whole, up_full, preferred_element_type=jnp.float32)

    def add_down(total, piece, start):
        columns = lax.dynamic_slice_in_dim(grads, start, piece.shape[1], 1)
        return total + lax.dot_general(
            columns, piece, (((1,), (1,)), ((), ())), preferred_element_type=jnp.float32
        )

    initial = jnp.zeros((whole.shape[0], down_weight.shape[0]), jnp.float32)
    hidden_grad = taken_in(down_weight, FSDP, (0, 1), 1, add_down, initial)
    squashed = jax.nn.sigmoid(gate)
    activated = gate * squashed
    slope = squashed * (1.0 + gate * (1.0 - squashed))
    hidden = (activated * up).astype(jnp.bfloat16)
    gate_delta = (hidden_grad * up * slope).astype(jnp.bfloat16)
    up_delta = (hidden_grad * activated).astype(jnp.bfloat16)

    def rows_term(start, count):
        gate_rows = lax.dynamic_slice_in_dim(gate_full, start, count, 0)
        up_rows = lax.dynamic_slice_in_dim(up_full, start, count, 0)
        first = lax.dot_general(
            gate_rows, gate_delta, (((1,), (1,)), ((), ())), preferred_element_type=jnp.float32
        )
        second = lax.dot_general(
            up_rows, up_delta, (((1,), (1,)), ((), ())), preferred_element_type=jnp.float32
        )
        return first + second

    local_rows = own_rows(rows_term, tokens.shape[1], "tp")
    input_grad = local_rows.T.astype(jnp.bfloat16)
    rows_here = gate_weight.shape[0]

    def joint_term(start, count):
        return jnp.concatenate(
            [
                column_term(whole, gate_delta, start, count, factor),
                column_term(whole, up_delta, start, count, factor),
                column_term(grads, hidden, start, count, factor),
            ],
            axis=1,
        )

    summed = own_rows(joint_term, rows_here, FSDP)
    width = gate_delta.shape[1]
    gate_grad = summed[:, :width]
    up_grad = summed[:, width : 2 * width]
    down_grad = summed[:, 2 * width :].T
    return (input_grad, gate_grad, up_grad, down_grad)


def solution(mesh):
    finer = Mesh(mesh.devices.reshape(2, 4, mesh.shape["tp"]), ("fsdp_0", "fsdp_1", "tp"))
    return jax.shard_map(
        shards,
        mesh=finer,
        in_specs=(P(FSDP, "tp"), P(FSDP, "tp"), P(FSDP, "tp"), P(FSDP, "tp"), P("tp", FSDP)),
        out_specs=(P(FSDP, "tp"), P(FSDP, "tp"), P(FSDP, "tp"), P("tp", FSDP)),
        check_vma=False,
    )
```

profile of v0, /device:TPU:0, one launch (start us, length us, event | category | flops | bytes accessed | tf_op | source)
XLA Modules:
  0.0 450.9 jit_solution(1478735136044264735)
XLA Ops:
  7.2 12.9 %all-gather.1 = bf16[256,1024]{1,0:T(8,128)(2,1)} all-gather(bf16[128,1024]{1,0:T(8,128)(2,1)} %param.9), channel_id=3, replica_groups=mesh['fsdp_0'=2,'fsdp_1'=4,'tp'=16] {'fsdp_0'}, dimensions={0}, use_global_device_ids=true | all-gather | bytes 786432 | tf_op jit(solution)/shard_map/all_gather | solution.py:30
  20.2 1.9 pad_maximum_fusion.1
  22.1 0.7 all-gather.11.cloned.1.call-update
  22.9 0.5 all-gather.7.cloned.1.call-update
  23.5 27.7 %all-gather.9.cloned.1.call-done = bf16[8,128,1024]{2,1,0:T(8,128)(2,1)} async-done(((bf16[2,128,1024]{2,1,0:T(8,128)(2,1)}), bf16[8,128,1024]{2,1,0:T(8,128)(2,1)}) %all-gather.9.cloned.1.call-update) | async-done | bytes 2097168 | tf_op jit(solution)/shard_map/all_gather | solution.py:30
  51.2 1.9 copy.27
  53.1 2.4 copy.28
  55.5 70.3 %all-gather.13.cloned.1.call-done = bf16[2097152]{0:T(1024)(128)(2,1)} async-done(((bf16[262144]{0:T(1024)(128)(2,1)}), bf16[2097152]{0:T(1024)(128)(2,1)}) %all-gather.13.cloned.1.call-update) | async-done | bytes 4194320 | tf_op jit(solution)/shard_map/all_gather | solution.py:19
  125.8 5.9 %reshape.28 = bf16[8,262144]{1,0:T(8,128)(2,1)} reshape(bf16[2097152]{0:T(1024)(128)(2,1)} %all-gather.13.cloned.1.call-done) | data formatting | bytes 8388608 | tf_op jit(solution)/shard_map/all_gather | solution.py:19
  131.7 3.9 fusion.6
  135.6 2.3 reshape_reshape.6
  137.9 2.6 reshape_reshape.7
  140.4 21.9 %all-gather.11.cloned.1.call-done = bf16[256,8192]{1,0:T(8,128)(2,1)} async-done(((bf16[256,512]{1,0:T(8,128)(2,1)}), bf16[256,8192]{1,0:T(8,128)(2,1)}) %all-gather.11.cloned.1.call-update) | async-done | bytes 4194320 | tf_op jit(solution)/shard_map/all_gather | solution.py:61
  162.3 4.2 convolution_bitcast_fusion
  166.6 1.3 convolution_bitcast_fusion.1
  167.9 33.2 %all-gather.7.cloned.1.call-done = bf16[256,8192]{1,0:T(8,128)(2,1)} async-done(((bf16[256,512]{1,0:T(8,128)(2,1)}), bf16[256,8192]{1,0:T(8,128)(2,1)}) %all-gather.7.cloned.1.call-update) | async-done | bytes 4194320 | tf_op jit(solution)/shard_map/all_gather | solution.py:62
  201.1 4.2 multiply_convert_fusion.1
  205.4 1.3 fusion.7
  206.6 4.5 convolution_add_fusion
  211.2 0.2 reduce-scatter.5.cloned.1.call-start
  211.4 3.3 fusion.1
  214.8 0.9 fusion.2
  215.8 1.3 copy-done.3
  217.0 1.0 fusion
  218.0 5.0 %pad_maximum_fusion = f32[8192,384]{0,1:T(8,128)} fusion(f32[8192,128]{0,1:T(8,128)S(1)} %fusion, f32[8192,128]{0,1:T(8,128)S(1)} %fusion.1, f32[8192,128]{0,1:T(8,128)S(1)} %fusion.2), kind=kLoop, calls=%fused_computation | loop fusion | flops 6291456 | bytes 25165824 | tf_op jit(solution)/shard_map/concatenate | solution.py:98
  223.0 63.3 %reduce-scatter.3.cloned.1.call-done = f32[512,256]{1,0:T(8,128)} async-done(((f32[8192,256]{1,0:T(8,128)}), f32[512,256]{1,0:T(8,128)}) %reduce-scatter.3.cloned.1.call-update) | async-done | bytes 524304 | tf_op jit(solution)/shard_map/reduce_scatter | solution.py:48
  286.3 1.1 convert_bitcast_fusion
  287.4 0.8 copy.31
  288.2 151.6 %reduce-scatter.5.cloned.1.call-done = f32[1024,384]{0,1:T(8,128)} async-done(((f32[8192,384]{0,1:T(8,128)}), f32[1024,384]{0,1:T(8,128)}) %reduce-scatter.5.cloned.1.call-update) | async-done | bytes 1572880 | tf_op jit(solution)/shard_map/reduce_scatter | solution.py:48
  439.8 2.3 slice_bitcast_fusion
  442.1 1.0 copy.32
  443.1 1.0 copy.33
  (16 shorter events, 0.5 us)
Async XLA Ops:
  7.2 44.0 %all-gather.9.cloned.1.call-start = ((), (), s32[]{:S(2)}) async-start(), calls=%async_computation.3 | async-start | bytes 2621440 | tf_op jit(solution)/shard_map/all_gather | solution.py:30
  20.2 105.7 %all-gather.13.cloned.1.call-start = ((), (), s32[]{:S(2)}) async-start(), calls=%async_computation.7 | async-start | bytes 4718592 | tf_op jit(solution)/shard_map/all_gather | solution.py:19
  22.1 140.2 %all-gather.11.cloned.1.call-start = ((), (), s32[]{:S(2)}) async-start(), calls=%async_computation.4 | async-start | bytes 4456448 | tf_op jit(solution)/shard_map/all_gather | solution.py:61
  22.8 178.3 %all-gather.7.cloned.1.call-start = ((), (), s32[]{:S(2)}) async-start(), calls=%async_computation.2 | async-start | bytes 4456448 | tf_op jit(solution)/shard_map/all_gather | solution.py:62
  23.4 262.9 %reduce-scatter.3.cloned.1.call-start = ((), (), s32[]{:S(2)}) async-start(), calls=%async_computation.5 | async-start | bytes 8912896 | tf_op jit(solution)/shard_map/reduce_scatter | solution.py:48
  162.3 4.2 copy-start
  201.1 4.3 copy-start.2
  211.2 228.6 %reduce-scatter.5.cloned.1.call-start = ((), (), s32[]{:S(2)}) async-start(), calls=%async_computation.6 | async-start | bytes 14155776 | tf_op jit(solution)/shard_map/reduce_scatter | solution.py:48
  211.4 3.5 copy-start.1
  214.8 2.2 copy-start.3
Sparse Core Ops, SparseCore 0:
  20.3 30.8 all-gather.8
  54.1 71.6 all-gather.12
  127.5 34.7 all-gather.10
  163.9 37.2 all-gather.6
  211.3 75.0 reduce-scatter.2
  290.1 149.6 reduce-scatter.4
where the time goes:
time: 451 us
  waiting for transfers between devices  369 us (82%)
  local copies, waits for them, and re-layouts  25.4 us (6%)
  matrix products  20.7 us (5%)
  between operations  14.2 us (3%)
  blocking collectives  12.9 us (3%)
  other arithmetic  7.91 us (2%)
    reduce_scatter x2, waiting for transfers between devices, own_rows(): lax.psum_scatter(portion(jnp.int32(0), count), axis, scatter_dimension=0,...  215 us
    all_gather x1, waiting for transfers between devices, one_gather(): lines, at, outs = (lax.all_gather(line, axis), 0, [])  70.3 us
    all_gather x1, waiting for transfers between devices, shards(): grads = lax.all_gather(out_grad, 'tp', axis=1, tiled=True)  33.2 us
    all_gather x1, waiting for transfers between devices, stacked_from(): parts = lax.all_gather(parts, axes[k], axis=0, tiled=True)  27.7 us
    all_gather x1, waiting for transfers between devices, shards(): whole = lax.all_gather(tokens, 'tp', axis=1, tiled=True)  21.9 us
    all_gather x1, blocking collectives, stacked_from(): parts = lax.all_gather(parts, axes[k], axis=0, tiled=True)  12.9 us
  transfers between devices with their start and end apart: 6, of which 6 were waited for; matrix products, arithmetic and copies ran while one was open for 9% of the time, Pallas kernels for 0%

commit v1 on v0

--- a/solution.py
+++ b/solution.py
@@ -4,6 +4,7 @@
 from jax import lax
 from jax.sharding import Mesh
 from jax.sharding import PartitionSpec as P
+from jax.lax import all_to_all, axis_size
 
 FSDP = ("fsdp_0", "fsdp_1")
 
@@ -59,7 +60,10 @@
 def shards(tokens, out_grad, gate_weight, up_weight, down_weight):
     factor = 1.0 / math.sqrt(tokens.shape[0] * lax.axis_size(FSDP))
     whole = lax.all_gather(tokens, "tp", axis=1, tiled=True)
-    grads = lax.all_gather(out_grad, "tp", axis=1, tiled=True)
+    view_slabs_on_mesh = lambda x_local: jnp.concatenate(
+        all_to_all(jnp.stack([x_local for _ in range(axis_size("tp"))], axis=0), "tp", 0, 0), axis=1
+    )
+    grads = view_slabs_on_mesh(out_grad)
     gate_full, up_full = one_gather((gate_weight, up_weight), FSDP, (0, 0))
     gate = jnp.dot(whole, gate_full, preferred_element_type=jnp.float32)
     up = jnp.dot(whole, up_full, preferred_element_type=jnp.float32)

time: 451 us -> 432 us (0.958)
  waiting for transfers between devices: 369 us -> 340 us
  starting transfers between devices: 0.42 us -> 5.29 us
    all_gather x1 -> x0, waiting for transfers between devices: 33.2 us -> none  [shards(): grads = lax.all_gather(out_grad, 'tp', axis=1, tiled=True)]
    all_gather x1, waiting for transfers between devices: 70.3 us -> 84.2 us  [one_gather(): lines, at, outs = (lax.all_gather(line, axis), 0, [])]
    all_gather x1, waiting for transfers between devices: 27.7 us -> 19.9 us  [stacked_from(): parts = lax.all_gather(parts, axes[k], axis=0, tiled=True)]
    all_to_all x0 -> x1, starting transfers between devices: none -> 4.91 us  [shards(): all_to_all(jnp.stack([x_local for _ in range(axis_size('tp'))], axis=0),...]
  transfers between devices with their start and end apart: 6 -> 6, of which waited for: 6 -> 5; matrix products, arithmetic and copies ran while one was open for 9% -> 10% of each run, Pallas kernels for 0% -> 0%
where the time goes in v1:
time: 432 us; the launch traced here: 431 us
  waiting for transfers between devices  340 us (79%)
  local copies, waits for them, and re-layouts  27.6 us (6%)
  matrix products  23.5 us (5%)
  between operations  13.9 us (3%)
  blocking collectives  12.9 us (3%)
  other arithmetic  7.89 us (2%)
  starting transfers between devices  5.29 us (1%)
    reduce_scatter x2, waiting for transfers between devices, own_rows(): lax.psum_scatter(portion(jnp.int32(0), count), axis, scatter_dimension=0,...  213 us
    all_gather x1, waiting for transfers between devices, one_gather(): lines, at, outs = (lax.all_gather(line, axis), 0, [])  84.2 us
    all_gather x1, waiting for transfers between devices, shards(): whole = lax.all_gather(tokens, 'tp', axis=1, tiled=True)  21.9 us
    all_gather x1, waiting for transfers between devices, stacked_from(): parts = lax.all_gather(parts, axes[k], axis=0, tiled=True)  19.9 us
    all_gather x1, blocking collectives, stacked_from(): parts = lax.all_gather(parts, axes[k], axis=0, tiled=True)  12.9 us
  transfers between devices with their start and end apart: 6, of which 5 were waited for; matrix products, arithmetic and copies ran while one was open for 10% of the time, Pallas kernels for 0%

profile of v1, /device:TPU:0, one launch (start us, length us, event | category | flops | bytes accessed | tf_op | source)
XLA Modules:
  0.0 431.4 jit_solution(13825007666663307642)
XLA Ops:
  7.2 12.9 %all-gather.1 = bf16[256,1024]{1,0:T(8,128)(2,1)} all-gather(bf16[128,1024]{1,0:T(8,128)(2,1)} %param.9), channel_id=3, replica_groups=mesh['fsdp_0'=2,'fsdp_1'=4,'tp'=16] {'fsdp_0'}, dimensions={0}, use_global_device_ids=true | all-gather | bytes 786432 | tf_op jit(solution)/shard_map/all_gather | solution.py:31
  20.2 1.9 pad_maximum_fusion.1
  22.1 1.1 copy.29
  23.2 2.4 stack.2
  25.6 4.9 %all-to-all-start = ((bf16[16,256,512]{1,2,0:T(8,128)(2,1)}), bf16[16,256,512]{1,2,0:T(8,128)(2,1)}, u32[]{:S(2)}, u32[]{:S(2)}) async-start(bf16[16,256,512]{1,2,0:T(8,128)(2,1)} %stack.2), calls=%async_computation | async-start | bytes 8388608 | tf_op jit(solution)/shard_map/all_to_all | solution.py:64
  30.5 0.7 all-gather.8.cloned.1.call-update
  31.3 19.9 %all-gather.6.cloned.1.call-done = bf16[8,128,1024]{2,1,0:T(8,128)(2,1)} async-done(((bf16[2,128,1024]{2,1,0:T(8,128)(2,1)}), bf16[8,128,1024]{2,1,0:T(8,128)(2,1)}) %all-gather.6.cloned.1.call-update) | async-done | bytes 2097168 | tf_op jit(solution)/shard_map/all_gather | solution.py:31
  51.2 1.9 copy.30
  53.1 2.4 copy.31
  55.5 84.2 %all-gather.10.cloned.1.call-done = bf16[2097152]{0:T(1024)(128)(2,1)} async-done(((bf16[262144]{0:T(1024)(128)(2,1)}), bf16[2097152]{0:T(1024)(128)(2,1)}) %all-gather.10.cloned.1.call-update) | async-done | bytes 4194320 | tf_op jit(solution)/shard_map/all_gather | solution.py:20
  139.7 5.9 %reshape.38 = bf16[8,262144]{1,0:T(8,128)(2,1)} reshape(bf16[2097152]{0:T(1024)(128)(2,1)} %all-gather.10.cloned.1.call-done) | data formatting | bytes 8388608 | tf_op jit(solution)/shard_map/all_gather | solution.py:20
  145.6 3.8 fusion.6
  149.4 2.3 reshape_reshape.6
  151.7 2.6 reshape_reshape.7
  154.3 21.9 %all-gather.8.cloned.1.call-done = bf16[256,8192]{1,0:T(8,128)(2,1)} async-done(((bf16[256,512]{1,0:T(8,128)(2,1)}), bf16[256,8192]{1,0:T(8,128)(2,1)}) %all-gather.8.cloned.1.call-update) | async-done | bytes 4194320 | tf_op jit(solution)/shard_map/all_gather | solution.py:62
  176.2 4.2 convolution_bitcast_fusion
  180.5 1.3 convolution_bitcast_fusion.1
  181.9 4.3 multiply_convert_fusion.1
  186.2 1.2 fusion.7
  187.4 4.5 %convolution_add_fusion = f32[8192,256]{1,0:T(8,128)} fusion(f32[8192,256]{1,0:T(8,128)S(1)} %fusion.7, bf16[8192,128]{1,0:T(8,128)(2,1)S(1)} %reshape_reshape.7, bf16[256,128]{1,0:T(8,128)(2,1)S(1)} %get-tuple-element.25), kind=kOutput, calls=%fused_computation.1 | convolution fusion | flops 538968064 | bytes 18939904 | tf_op jit(solution)/shard_map/dot_general | solution.py:92
  191.9 0.2 reduce-scatter.5.cloned.1.call-start
  192.2 3.3 fusion.1
  195.6 0.9 fusion.2
  196.6 3.7 fusion
  200.3 5.0 %pad_maximum_fusion = f32[8192,384]{0,1:T(8,128)} fusion(f32[8192,128]{0,1:T(8,128)S(1)} %fusion, f32[8192,128]{0,1:T(8,128)S(1)} %fusion.1, f32[8192,128]{0,1:T(8,128)S(1)} %fusion.2), kind=kLoop, calls=%fused_computation | loop fusion | flops 6291456 | bytes 25165824 | tf_op jit(solution)/shard_map/concatenate | solution.py:102
  205.3 61.9 %reduce-scatter.3.cloned.1.call-done = f32[512,256]{1,0:T(8,128)} async-done(((f32[8192,256]{1,0:T(8,128)}), f32[512,256]{1,0:T(8,128)}) %reduce-scatter.3.cloned.1.call-update) | async-done | bytes 524304 | tf_op jit(solution)/shard_map/reduce_scatter | solution.py:49
  267.1 1.1 convert_bitcast_fusion
  268.2 0.8 copy.34
  269.0 151.6 %reduce-scatter.5.cloned.1.call-done = f32[1024,384]{0,1:T(8,128)} async-done(((f32[8192,384]{0,1:T(8,128)}), f32[1024,384]{0,1:T(8,128)}) %reduce-scatter.5.cloned.1.call-update) | async-done | bytes 1572880 | tf_op jit(solution)/shard_map/reduce_scatter | solution.py:49
  420.6 2.3 slice_bitcast_fusion
  422.9 1.0 copy.35
  423.9 1.0 copy.36
  (15 shorter events, 0.4 us)
Async XLA Ops:
  7.2 44.0 %all-gather.6.cloned.1.call-start = ((), (), s32[]{:S(2)}) async-start(), calls=%async_computation.3 | async-start | bytes 2621440 | tf_op jit(solution)/shard_map/all_gather | solution.py:31
  20.2 119.5 %all-gather.10.cloned.1.call-start = ((), (), s32[]{:S(2)}) async-start(), calls=%async_computation.7 | async-start | bytes 4718592 | tf_op jit(solution)/shard_map/all_gather | solution.py:20
  25.6 156.3 %all-to-all-start = ((bf16[16,256,512]{1,2,0:T(8,128)(2,1)}), bf16[16,256,512]{1,2,0:T(8,128)(2,1)}, u32[]{:S(2)}, u32[]{:S(2)}) async-start(bf16[16,256,512]{1,2,0:T(8,128)(2,1)} %stack.2), calls=%async_computation | async-start | bytes 8388608 | tf_op jit(solution)/shard_map/all_to_all | solution.py:64
  30.5 145.7 %all-gather.8.cloned.1.call-start = ((), (), s32[]{:S(2)}) async-start(), calls=%async_computation.4 | async-start | bytes 4456448 | tf_op jit(solution)/shard_map/all_gather | solution.py:62
  31.2 235.9 %reduce-scatter.3.cloned.1.call-start = ((), (), s32[]{:S(2)}) async-start(), calls=%async_computation.5 | async-start | bytes 8912896 | tf_op jit(solution)/shard_map/reduce_scatter | solution.py:49
  176.2 4.3 copy-start
  181.8 4.3 %copy-start.2 = (bf16[8192,128]{1,0:T(8,128)(2,1)S(1)}, bf16[8192,128]{1,0:T(8,128)(2,1)}, u32[]{:S(2)}) copy-start(bf16[8192,128]{1,0:T(8,128)(2,1)} %reshape_reshape.6) | copy-start | bytes 6291460
  191.9 228.7 %reduce-scatter.5.cloned.1.call-start = ((), (), s32[]{:S(2)}) async-start(), calls=%async_computation.6 | async-start | bytes 14155776 | tf_op jit(solution)/shard_map/reduce_scatter | solution.py:49
  192.2 3.5 copy-start.1
Sparse Core Ops, SparseCore 0:
  20.3 30.8 all-gather.5
  54.1 85.5 all-gather.9
  141.4 34.7 all-gather.7
  192.1 75.0 reduce-scatter.2
  270.9 149.6 reduce-scatter.4
